TPU v7x, 32 devices: a 4x4x1 block of a 4x4x8 slice. The times are simulated.
32 devices in a mesh: dp: 1 (over z), tp: 4 (over y), ep: 8 (over x, core).
Axes of the slice: x: 4, y: 4, z: 1, core: 2. Of those that a mesh axis runs over, the one named last changes fastest.
The devices are a block of a 4x4x8 slice.
Arguments:
- x: bfloat16 [4096, 2048], P(('dp', 'ep', 'tp'))
- idx: int32 [4096, 8], P(('dp', 'ep', 'tp'))
- gate: float32 [4096, 8], P(('dp', 'ep', 'tp'))
- w1: bfloat16 [128, 2048, 768], P('ep', None, 'tp')
- w3: bfloat16 [128, 2048, 768], P('ep', None, 'tp')
- w2: bfloat16 [128, 768, 2048], P('ep', 'tp')
Outputs:
- output: bfloat16 [4096, 2048], P(('dp', 'ep', 'tp'))
All inputs are finite; a program needn't handle non-finite values.
Results may differ from a plain program's by a relative error of at most 0.001.
Values are sent between devices in bfloat16 or wider.
A program may use at most 768 MiB of HBM per device.

v0:
```python
import jax
import jax.numpy as jnp
from jax import lax
from jax.sharding import PartitionSpec as P


def _groups(idx, gate, lo, n_exp, cap):
    k = idx.shape[1]
    flat = idx.reshape(-1) - lo
    key = jnp.where((flat >= 0) & (flat < n_exp), flat, n_exp)
    order = jnp.argsort(key)
    counts = jnp.zeros((n_exp + 1,), jnp.int32).at[key].add(1)[:n_exp]
    starts = jnp.cumsum(counts) - counts
    slot = jnp.arange(cap)
    pid = order[jnp.clip(starts[:, None] + slot[None, :], 0, flat.shape[0] - 1)]
    g = jnp.where(slot[None, :] < counts[:, None], gate.reshape(-1)[pid], 0.0)
    return pid // k, g


def _experts(x, tok, g, w1, w3, w2):
    xg = x[tok]
    a = jnp.einsum('ecd,edf->ecf', xg, w1, preferred_element_type=jnp.float32)
    b = jnp.einsum('ecd,edf->ecf', xg, w3, preferred_element_type=jnp.float32)
    h = (jax.nn.silu(a) * b).astype(jnp.bfloat16)
    o = jnp.einsum('ecf,efd->ecd', h, w2, preferred_element_type=jnp.float32) * g[..., None]
    d = x.shape[1]
    return jnp.zeros(x.shape, jnp.float32).at[tok.reshape(-1)].add(o.reshape(-1, d))


def solution(mesh):
    n_pos = mesh.shape['ep']
    rows_spec = P(('dp', 'ep', 'tp'), None)

    def body(x, idx, gate, w1, w3, w2):
        xa = lax.all_gather(x, ('ep', 'tp'), axis=0, tiled=True)
        ia = lax.all_gather(idx, ('ep', 'tp'), axis=0, tiled=True)
        ga = lax.all_gather(gate, ('ep', 'tp'), axis=0, tiled=True)
        rows = xa.shape[0]
        n_exp, k = w1.shape[0], idx.shape[1]
        cap = 8 * ((k * rows // (n_exp * n_pos) + 9) // 8)
        lo = lax.axis_index('ep') * n_exp
        tok, g = _groups(ia, ga, lo, n_exp, cap)
        part = _experts(xa, tok, g, w1, w3, w2)
        y = lax.psum_scatter(part, ('ep', 'tp'), scatter_dimension=0, tiled=True)
        return y.astype(jnp.bfloat16)

    return jax.shard_map(body, mesh=mesh,
                         in_specs=(rows_spec, rows_spec, rows_spec,
                                   P('ep', None, 'tp'), P('ep', None, 'tp'), P('ep', 'tp', None)),
                         out_specs=rows_spec, check_vma=False)
```

profile of v0, /device:TPU:97, one launch (start us, length us, event | category | flops | bytes accessed | tf_op | source)
XLA Modules:
  0.0 687.4 jit_solution(5852441600650694742)
XLA Ops:
  6.5 0.0 all-gather.2.cloned.1.call-start
  6.6 0.7 all-gather.2.cloned.1.call-update
  7.3 0.1 reduce-scatter.2.cloned.1.call-start
  7.4 32.8 %all_gather.9 = s32[4096,8]{0,1:T(8,128)S(1)} all-gather(s32[128,8]{0,1:T(8,128)} %param.7), channel_id=1, replica_groups=mesh['dp'=1,'tp'=4,'ep'=8] {'ep','tp'}, dimensions={0}, use_global_device_ids=true | all-gather | bytes 135168 | tf_op jit(solution)/shard_map/all_gather | solution.py:36
  40.2 0.6 copy.8
  40.8 1.1 sub.33
  41.9 1.0 sub.32
  42.9 0.2 compare_select_fusion
  43.2 226.8 %scatter_custom_fusion = s32[17]{0:T(128)S(1)} fusion(s32[32768]{0:T(1024)S(1)} %bitcast.18, s32[32768]{0:T(1024)S(1)} %broadcast.281, s32[]{:T(128)} %constant.16.clone.1), kind=kCustom, calls=%fused_computation.36 | custom fusion | flops 32768 | bytes 72 | tf_op jit(solution)/shard_map/scatter-add | solution.py:12
  270.0 0.1 copy.10
  270.1 0.1 reduce
  270.2 0.1 compare_select_fusion.3
  270.3 0.1 reshape.290
  270.5 11.2 %sort.17 = (s32[32768]{0:T(1024)}, s32[32768]{0:T(1024)S(1)}) sort(s32[32768]{0:T(1024)S(1)} %and_select_fusion.1, s32[32768]{0:T(1024)S(1)} %iota.14), dimensions={0}, to_apply=%region_0.1 | sort | flops 491520 | bytes 524288 | tf_op jit(solution)/shard_map/jit(argsort)/sort | solution.py:11
  281.7 0.0 copy-start
  281.7 22.2 %gather_fusion = s32[4224]{0:T(1024)S(1)} fusion(s32[32768]{0:T(1024)S(1)} %get-tuple-element.6, s32[5120]{0:T(1024)S(1)} %pad_clamp_fusion.2), kind=kCustom, calls=%fused_computation | custom fusion | bytes 50688 | tf_op jit(solution)/shard_map/gather | solution.py:15
  303.9 0.1 gather.15
  304.0 0.1 reshape.298
  304.1 0.1 reshape.306
  304.2 0.0 copy-done
  304.2 33.0 %all_gather.11 = f32[4096,8]{0,1:T(8,128)S(1)} all-gather(f32[128,8]{0,1:T(8,128)S(1)} %copy-done), channel_id=1, replica_groups=mesh['dp'=1,'tp'=4,'ep'=8] {'ep','tp'}, dimensions={0}, use_global_device_ids=true | all-gather | bytes 135168 | tf_op jit(solution)/shard_map/all_gather | solution.py:37
  337.2 0.6 copy.11
  337.8 1.0 reshape.286
  338.8 22.2 %gather_fusion.2 = f32[4224]{0:T(1024)S(1)} fusion(f32[32768]{0:T(1024)S(1)} %reshape.286, s32[5120]{0:T(1024)S(1)} %pad_clamp_fusion), kind=kCustom, calls=%fused_computation.2 | custom fusion | bytes 50688 | tf_op jit(solution)/shard_map/gather | solution.py:16
  361.0 0.1 reshape.305
  361.1 0.1 fusion.8
  361.2 0.1 fusion.7
  361.3 0.0 all-gather.2.cloned.1.call-done
  361.3 41.0 %gather_fusion.1 = bf16[4224,2048]{1,0:T(8,128)(2,1)} fusion(bf16[4096,2048]{1,0:T(8,128)(2,1)} %all-gather.2.cloned.1.call-done, s32[5120]{0:T(1024)S(1)} %pad_clamp_fusion.1), kind=kCustom, calls=%fused_computation.1 | custom fusion | bytes 34619904 | tf_op jit(solution)/shard_map/gather | solution.py:21
  402.3 16.6 %fusion.13 = f32[16,264,192]{2,1,0:T(8,128)} fusion(bf16[16,264,2048]{2,1,0:T(8,128)(2,1)} %bitcast.16, bf16[16,2048,192]{1,2,0:T(8,128)(2,1)} %param.9), kind=kOutput, calls=%fused_computation.42 | convolution fusion | flops 3321888768 | bytes 33128448 | tf_op jit(solution)/shard_map/ecd,edf->ecf/dot_general | solution.py:22
  418.9 27.3 %broadcast_multiply_fusion = f32[16,264,2048]{2,1,0:T(8,128)} fusion(f32[16,264]{1,0:T(8,128)S(1)} %fusion.7, bf16[16,192,2048]{2,1,0:T(8,128)(2,1)} %param.11, f32[16,264,192]{2,1,0:T(8,128)} %fusion.13, bf16[16,264,2048]{2,1,0:T(8,128)(2,1)} %bitcast.17, bf16[16,2048,192]{1,2,0:T(8,128)(2,1)} %param.10), kind=kOutput, calls=%fused_computation.5 | convolution fusion | flops 6657294336 | bytes 80331264 | tf_op jit(solution)/shard_map/ecf,efd->ecd/dot_general | solution.py:25
  446.2 71.5 %scatter_custom_fusion.1 = f32[4096,2048]{1,0:T(8,128)} fusion(s32[4224]{0:T(1024)S(1)} %fusion.8, f32[4224,2048]{1,0:T(8,128)} %bitcast.19, f32[]{:T(128)} %constant.13.clone.1), kind=kCustom, calls=%fused_computation.6 | custom fusion | flops 8650752 | bytes 33554944 | tf_op jit(solution)/shard_map/scatter-add | solution.py:27
  517.7 0.1 reduce-scatter.2.cloned.1.call-update
  517.8 160.5 %reduce-scatter.2.cloned.1.call-done = f32[128,2048]{1,0:T(8,128)} async-done(((f32[4096,2048]{1,0:T(8,128)}), f32[128,2048]{1,0:T(8,128)}) %reduce-scatter.2.cloned.1.call-update) | async-done | bytes 1048592 | tf_op jit(solution)/shard_map/reduce_scatter | solution.py:44
  678.3 2.1 convert_element_type.7
  (11 shorter events, 0.1 us)
Async XLA Ops:
  6.5 354.8 %all-gather.2.cloned.1.call-start = ((), (), s32[]{:S(2)}) async-start(), calls=%async_computation.1 | async-start | bytes 17301504 | tf_op jit(solution)/shard_map/all_gather | solution.py:35
  7.3 671.0 %reduce-scatter.2.cloned.1.call-start = ((), (), s32[]{:S(2)}) async-start(), calls=%async_computation.2 | async-start | bytes 34603008 | tf_op jit(solution)/shard_map/reduce_scatter | solution.py:44
  281.7 22.5 %copy-start = (f32[128,8]{0,1:T(8,128)S(1)}, f32[128,8]{0,1:T(8,128)}, u32[]{:S(2)}) copy-start(f32[128,8]{0,1:T(8,128)} %param.8) | copy-start | bytes 12292
Sparse Core Ops, SparseCore 0:
  9.4 71.6 all-gather.1
  517.9 160.3 reduce-scatter.1
where the time goes:
time: 693 us; the launch traced here: 687 us
  other arithmetic  312 us (45%)
  waiting for transfers between devices  161 us (23%)
  local copies, waits for them, and re-layouts  90.3 us (13%)
  blocking collectives  65.8 us (9%)
  matrix products  43.9 us (6%)
  between operations  13.8 us (2%)
    scatter-add x1, other arithmetic, _groups(): counts = jnp.zeros((n_exp + 1,), jnp.int32).at[key].add(1)[:n_exp]  227 us
    reduce_scatter x1, waiting for transfers between devices, body(): y = lax.psum_scatter(part, ('ep', 'tp'), scatter_dimension=0, tiled=True)  160 us
    scatter-add x1, other arithmetic, _experts(): jnp.zeros(x.shape, jnp.float32).at[tok.reshape(-1)].add(o.reshape(-1, d))  71.5 us
    gather x1, local copies, waits for them, and re-layouts, _experts(): xg = x[tok]  41 us
    all_gather x1, blocking collectives, body(): ga = lax.all_gather(gate, ('ep', 'tp'), axis=0, tiled=True)  33 us
    all_gather x1, blocking collectives, body(): ia = lax.all_gather(idx, ('ep', 'tp'), axis=0, tiled=True)  32.8 us
    dot_general x1, matrix products, _experts(): jnp.einsum('ecf,efd->ecd', h, w2, preferred_element_type=jnp.float32)  27.3 us
    gather x2, local copies, waits for them, and re-layouts, _groups(): pid = order[jnp.clip(starts[:, None] + slot[None, :], 0, flat.shape[0] - 1)]  22.3 us
  transfers between devices with their start and end apart: 2, of which 1 were waited for; matrix products, arithmetic and copies ran while one was open for 42% of the time, Pallas kernels for 0%

commit v1 on v0

v1 whole, which is shorter than its diff:
```python
import functools

import jax
import jax.numpy as jnp
from jax import lax
from jax.experimental import pallas as pl
from jax.experimental.pallas import tpu as pltpu
from jax.sharding import PartitionSpec as P

MESH = pl.DeviceIdType.MESH
GATE_LANES = 128
SLOTS = 3


def _route(x, idx, gate, n_pos, n_exp, cap):
    rows = x.shape[0]
    pos = idx // n_exp
    hit = jnp.any(pos[:, None, :] == jnp.arange(n_pos)[None, :, None], axis=-1)
    r = jnp.arange(rows)
    before = (r[None, :] < r[:, None]).astype(jnp.bfloat16)
    rank = jnp.dot(before, hit.astype(jnp.bfloat16), preferred_element_type=jnp.float32).astype(jnp.int32)
    slot = jnp.where(hit, rank, cap)
    sel = slot.T[:, None, :] == jnp.arange(cap)[None, :, None]
    pick = sel.astype(jnp.bfloat16)
    xs = jnp.einsum('qsr,rd->qsd', pick, x, preferred_element_type=jnp.float32).astype(jnp.bfloat16)
    experts = jnp.arange(n_pos * n_exp)
    g = jnp.sum(jnp.where(idx[:, :, None] == experts[None, None, :], gate[:, :, None], 0.0), axis=1)
    hi = lax.reduce_precision(g, 8, 7)
    mid = lax.reduce_precision(g - hi, 8, 7)
    lo = g - hi - mid
    parts = jnp.stack([hi, mid, lo], axis=1).astype(jnp.bfloat16).reshape(rows, 3, n_pos, n_exp)
    gs = jnp.einsum('qsr,rpqe->qspe', pick, parts, preferred_element_type=jnp.float32)
    gs = gs.reshape(n_pos, cap, 3 * n_exp).astype(jnp.bfloat16)
    gs = jnp.pad(gs, ((0, 0), (0, 0), (0, GATE_LANES - 3 * n_exp)))
    return jnp.concatenate([xs, gs], axis=-1), sel


def _kernel(n_pos, n_tp, cap, xs, w1, w3, w2, out, xb, acc, rec, rel, b1, b3, b2,
            wsem, sx, rx, sy, ry, sr, rr, sc, rc, sf, rf):
    q = lax.axis_index('ep')
    y = lax.axis_index('tp')
    up = lax.rem(y + 1, n_tp)
    down = lax.rem(y + n_tp - 1, n_tp)
    n_exp, d, ff = w1.shape
    ch = n_pos * cap
    half = ch // 2
    steps = 4 * n_exp

    def weights(step):
        e, s = lax.rem(step, n_exp), lax.rem(step, SLOTS)
        return (pltpu.make_async_copy(w1.at[e], b1.at[s], wsem.at[s, 0]),
                pltpu.make_async_copy(w3.at[e], b3.at[s], wsem.at[s, 1]),
                pltpu.make_async_copy(w2.at[e], b2.at[s], wsem.at[s, 2]))

    def remote(src, dst, ssem, rsem, dev):
        return pltpu.make_async_remote_copy(src_ref=src, dst_ref=dst, send_sem=ssem, recv_sem=rsem,
                                            device_id=dev, device_id_type=MESH)

    for s in range(SLOTS - 1):
        for c in weights(s):
            c.start()

    barrier = pltpu.get_barrier_semaphore()
    for k in range(1, n_pos):
        pl.semaphore_signal(barrier, inc=1, device_id={'ep': lax.rem(q + k, n_pos)}, device_id_type=MESH)
    for t in (up, down):
        pl.semaphore_signal(barrier, inc=1, device_id={'tp': t}, device_id_type=MESH)
    pl.semaphore_wait(barrier, n_pos + 1)

    def blk(k):
        return pl.ds(k * cap, cap)

    def x_send(k):
        to = lax.rem(q + n_pos - k, n_pos)
        return remote(xs.at[to], xb.at[0, blk(k)], sx.at[k], rx.at[k], {'ep': to})

    def y_send(way, k):
        src = xs.at[q] if k == 0 else xb.at[0, blk(k)]
        if way == 0:
            return remote(src, xb.at[3, blk(k)], sy.at[0, k], ry.at[0, k], {'tp': up})
        return remote(src, xb.at[1, blk(k)], sy.at[1, k], ry.at[1, k], {'tp': down})

    def y_got(way, k):
        j = 3 if way == 0 else 1
        return remote(xb.at[j, blk(k)], xb.at[j, blk(k)], sy.at[way, k], ry.at[way, k], {'tp': up})

    def relay(way, i):
        if way == 1:
            b = blk(2 * i)
            return remote(xb.at[1, b], xb.at[2, b], sr.at[1, i], rr.at[1, i], {'tp': down})
        b = blk(2 * i + 1)
        return remote(xb.at[3, b], xb.at[2, b], sr.at[0, i], rr.at[0, i], {'tp': up})

    for k in range(1, n_pos):
        x_send(k).start()
    y_send(0, 0).start()
    y_send(1, 0).start()
    xb[0, blk(0)] = xs[q]
    for k in range(1, n_pos):
        x_send(k).wait_recv()
        y_send(0, k).start()
        y_send(1, k).start()

    lane = lax.broadcasted_iota(jnp.int32, (ch, GATE_LANES), 1)

    def chunk(j, order, hook=None):
        acc[j] = jnp.zeros((ch, d), jnp.float32)

        def expert(e, carry):
            step = order * n_exp + e
            s = lax.rem(step, SLOTS)

            @pl.when(step + SLOTS - 1 < steps)
            def _():
                for c in weights(step + SLOTS - 1):
                    c.start()
            for c in weights(step):
                c.wait()
            if hook is not None:
                hook(e)
            xv = xb[j, :, 0:d]
            a = jnp.dot(xv, b1[s], preferred_element_type=jnp.float32)
            b = jnp.dot(xv, b3[s], preferred_element_type=jnp.float32)
            h = (a * jax.nn.sigmoid(a) * b).astype(jnp.bfloat16)
            gv = xb[j, :, d:d + GATE_LANES].astype(jnp.float32)
            mine = (lane == e) | (lane == e + n_exp) | (lane == e + 2 * n_exp)
            g = jnp.sum(jnp.where(mine, gv, 0.0), axis=1, keepdims=True)
            wide = d // 4
            for n in range(4):
                cols = pl.ds(n * wide, wide)
                o = jnp.dot(h, b2[s, :, cols], preferred_element_type=jnp.float32)
                acc[j, :, cols] += g * o
            return carry

        lax.fori_loop(0, n_exp, expert, 0)

    quarter = n_exp // 4

    def relays(e):
        @pl.when(lax.rem(e, quarter) == quarter - 1)
        def _():
            i = e // quarter
            y_got(1, 2 * i).wait_recv()
            relay(1, i).start()
            y_got(0, 2 * i + 1).wait_recv()
            relay(0, i).start()

    lo, hi = pl.ds(0, half), pl.ds(half, half)

    c_up_hi = remote(acc.at[1, hi], rec.at[0, hi], sc.at[0], rc.at[0], {'tp': up})
    c_up_lo = remote(acc.at[1, lo], rec.at[0, lo], sc.at[1], rc.at[1], {'tp': up})
    c_dn_lo = remote(acc.at[3, lo], rec.at[1, lo], sc.at[2], rc.at[2], {'tp': down})
    c_dn_hi = remote(acc.at[3, hi], rec.at[1, hi], sc.at[3], rc.at[3], {'tp': down})
    c_far_lo = remote(acc.at[2, lo], rel.at[0], sc.at[4], rc.at[4], {'tp': up})
    c_far_hi = remote(acc.at[2, hi], rel.at[1], sc.at[5], rc.at[5], {'tp': down})

    chunk(0, 0, relays)
    for i in range(n_pos // 2):
        y_got(1, 2 * i + 1).wait_recv()
    chunk(1, 1)
    c_up_hi.start()
    for i in range(n_pos // 2):
        relay(0, i).wait_recv()
        relay(1, i).wait_recv()
    chunk(2, 2)
    c_far_lo.start()
    c_far_hi.start()
    for i in range(n_pos // 2):
        y_got(0, 2 * i).wait_recv()
    chunk(3, 3)
    c_dn_lo.start()
    c_far_lo.wait_recv()
    acc[1, lo] += rel[0]
    c_up_lo.start()
    c_far_hi.wait_recv()
    acc[3, hi] += rel[1]
    c_dn_hi.start()

    def f_send(k):
        to = lax.rem(q + k, n_pos)
        return remote(acc.at[0, blk(k)], out.at[q], sf.at[k], rf.at[k], {'ep': to})

    c_dn_lo.wait_recv()
    c_up_lo.wait_recv()
    acc[0, lo] += rec[0, lo] + rec[1, lo]
    for k in range(1, n_pos // 2):
        f_send(k).start()
    out[q] = acc[0, blk(0)]
    c_up_hi.wait_recv()
    c_dn_hi.wait_recv()
    acc[0, hi] += rec[0, hi] + rec[1, hi]
    for k in range(n_pos // 2, n_pos):
        f_send(k).start()

    for k in range(1, n_pos):
        x_send(k).wait_send()
    for k in range(n_pos):
        y_send(0, k).wait_send()
        y_send(1, k).wait_send()
    for i in range(n_pos // 2):
        relay(0, i).wait_send()
        relay(1, i).wait_send()
    for c in (c_up_hi, c_up_lo, c_dn_lo, c_dn_hi, c_far_lo, c_far_hi):
        c.wait_send()
    for k in range(1, n_pos):
        f_send(k).wait_send()
        f_send(k).wait_recv()


def _moe(xs, w1, w3, w2, n_pos, n_tp, cap):
    n_exp, d, ff = w1.shape
    ch = n_pos * cap
    wide = xs.shape[-1]
    dma = pltpu.SemaphoreType.DMA
    vmem = pl.BlockSpec(memory_space=pltpu.VMEM)
    hbm = pl.BlockSpec(memory_space=pl.ANY)
    return pl.pallas_call(
        functools.partial(_kernel, n_pos, n_tp, cap),
        out_shape=jax.ShapeDtypeStruct((n_pos, cap, d), jnp.float32),
        in_specs=[vmem, hbm, hbm, hbm],
        out_specs=vmem,
        scratch_shapes=[
            pltpu.VMEM((4, ch, wide), jnp.bfloat16),
            pltpu.VMEM((4, ch, d), jnp.float32),
            pltpu.VMEM((2, ch, d), jnp.float32),
            pltpu.VMEM((2, ch // 2, d), jnp.float32),
            pltpu.VMEM((SLOTS, d, ff), jnp.bfloat16),
            pltpu.VMEM((SLOTS, d, ff), jnp.bfloat16),
            pltpu.VMEM((SLOTS, ff, d), jnp.bfloat16),
            dma((SLOTS, 3)),
            dma((n_pos,)), dma((n_pos,)),
            dma((2, n_pos)), dma((2, n_pos)),
            dma((2, n_pos // 2)), dma((2, n_pos // 2)),
            dma((6,)), dma((6,)),
            dma((n_pos,)), dma((n_pos,)),
        ],
        compiler_params=pltpu.CompilerParams(
            collective_id=0, has_side_effects=True, vmem_limit_bytes=60 * 1024 * 1024),
    )(xs, w1, w3, w2)


def solution(mesh):
    n_pos, n_tp = mesh.shape['ep'], mesh.shape['tp']
    rows_spec = P(('dp', 'ep', 'tp'), None)

    def body(x, idx, gate, w1, w3, w2):
        rows, d = x.shape
        n_exp = w1.shape[0]
        cap = 2 * rows // n_pos
        xs, sel = _route(x, idx, gate, n_pos, n_exp, cap)
        back = _moe(xs, w1, w3, w2, n_pos, n_tp, cap)
        y = jnp.einsum('qsr,qsd->rd', sel.astype(jnp.float32), back,
                       precision=lax.Precision.HIGHEST, preferred_element_type=jnp.float32)
        return y.astype(jnp.bfloat16)

    return jax.shard_map(body, mesh=mesh,
                         in_specs=(rows_spec, rows_spec, rows_spec,
                                   P('ep', None, 'tp'), P('ep', None, 'tp'), P('ep', 'tp', None)),
                         out_specs=rows_spec, check_vma=False)
```

time: 693 us -> 213 us (0.31)
  other arithmetic: 312 us -> 2.24 us
  Pallas kernels: 0 us -> 162 us
  waiting for transfers between devices: 161 us -> 0 us
  blocking collectives: 65.8 us -> 0 us
  local copies, waits for them, and re-layouts: 90.3 us -> 43 us
  matrix products: 43.9 us -> 4.03 us
  between operations: 13.8 us -> 0.07 us
    scatter-add x2 -> x0, other arithmetic: 298 us -> none  [the longest x1 227 us: _groups(): counts = jnp.zeros((n_exp + 1,), jnp.int32).at[key].add(1)[:n_exp]]
    pallas_call x0 -> x1, Pallas kernels: none -> 162 us  [_moe(): pl.pallas_call(functools.partial(_kernel, n_pos, n_tp, cap), out_shape=ja...]
    reduce_scatter x1 -> x0, waiting for transfers between devices: 160 us -> none  [body(): y = lax.psum_scatter(part, ('ep', 'tp'), scatter_dimension=0, tiled=True)]
    gather x5 -> x0, local copies, waits for them, and re-layouts: 85.5 us -> none  [the longest x1 41 us: _experts(): xg = x[tok]]
    all_gather x2 -> x0, blocking collectives: 65.8 us -> none  [the longest x1 33 us: body(): ga = lax.all_gather(gate, ('ep', 'tp'), axis=0, tiled=True)]
    unnamed x2 -> x8, local copies, waits for them, and re-layouts: 0.01 us -> 42.8 us
    dot_general x2 -> x4, matrix products: 43.9 us -> 4.03 us  [the longest x1 3.29 us: body(): jnp.einsum('qsr,qsd->rd', sel.astype(jnp.float32), back, precision=lax.Pr...]
    sort x1 -> x0, other arithmetic: 11.2 us -> none  [_groups(): order = jnp.argsort(key)]
  transfers between devices with their start and end apart: 2 -> 0, of which waited for: 1 -> 0; matrix products, arithmetic and copies ran while one was open for 42% -> 0% of each run, Pallas kernels for 0% -> 0%
where the time goes in v1:
time: 213 us; the launch traced here: 212 us
  Pallas kernels  162 us (76%)
  local copies, waits for them, and re-layouts  43 us (20%)
  matrix products  4.03 us (2%)
  other arithmetic  2.24 us (1%)
    pallas_call x1, Pallas kernels, _moe(): pl.pallas_call(functools.partial(_kernel, n_pos, n_tp, cap), out_shape=ja...  162 us
    unnamed x8, local copies, waits for them, and re-layouts  42.8 us

profile of v1, /device:TPU:97, one launch (start us, length us, event | category | flops | bytes accessed | tf_op | source)
XLA Modules:
  0.0 211.7 jit_solution(8241740082523849512)
XLA Ops:
  0.0 0.0 copy-start
  0.0 0.8 add_select_fusion
  0.8 0.1 fusion.3
  0.9 0.8 copy.20
  1.7 0.8 copy.19
  2.5 0.3 select_reduce_fusion
  2.9 0.1 copy.21
  3.0 0.2 convolution_convert_fusion.1
  3.2 0.1 copy.22
  3.3 0.0 copy-done
  3.3 0.4 convolution_convert_fusion
  3.7 1.1 fusion.2.xs
  4.8 20.6 %copy.23.w1 = bf16[16,2048,192]{2,1,0:T(8,128)(2,1)} copy(bf16[16,2048,192]{1,2,0:T(8,128)(2,1)} %param.9) | data formatting | bytes 25165824 | tf_op args[3]
  25.4 20.6 %copy.24.w3 = bf16[16,2048,192]{2,1,0:T(8,128)(2,1)} copy(bf16[16,2048,192]{1,2,0:T(8,128)(2,1)} %param.10) | data formatting | bytes 25165824 | tf_op args[4]
  46.0 0.0 copy-start.1
  46.0 162.4 %shard_map.64 = f32[8,32,2048]{2,1,0:T(8,128)} custom-call(bf16[8,32,2176]{2,1,0:T(8,128)(2,1)} %fusion.2.xs, bf16[16,2048,192]{2,1,0:T(8,128)(2,1)} %copy.23.w1, bf16[16,2048,192]{2,1,0:T(8,128)(2,1)} %copy.24.w3, bf16[16,192,2048]{2,1,0:T(8,128)(2,1)} %w2.1), custom_call_target="tpu_custom_call" | custom-call | tf_op jit(solution)/shard_map/pallas_call | solution.py:217
  208.4 3.3 %fusion = bf16[128,2048]{1,0:T(8,128)(2,1)} fusion(f32[8,32,2048]{2,1,0:T(8,128)} %shard_map.64, s32[8,128]{1,0:T(8,128)S(1)} %fusion.3), kind=kOutput, calls=%fused_computation.2 | convolution fusion | flops 805601280 | bytes 2625536 | tf_op jit(solution)/shard_map/qsr,qsd->rd/dot_general | solution.py:252
  211.7 0.0 copy-done.1
  (2 shorter events, 0.0 us)
Async XLA Ops:
  0.0 3.3 %copy-start = (bf16[128,2048]{1,0:T(8,128)(2,1)S(1)}, bf16[128,2048]{1,0:T(8,128)(2,1)}, u32[]{:S(2)}) copy-start(bf16[128,2048]{1,0:T(8,128)(2,1)} %param.6) | copy-start | bytes 1572868
  46.0 165.7 %copy-start.1 = (bf16[128,2048]{1,0:T(8,128)(2,1)S(1)}, bf16[128,2048]{1,0:T(8,128)(2,1)}, u32[]{:S(2)}) copy-start(bf16[128,2048]{1,0:T(8,128)(2,1)} %param.6) | copy-start | bytes 1572868

commit v2 on v0

v2 whole, which is shorter than its diff:
```python
import functools

import jax
import jax.numpy as jnp
from jax import lax
from jax.experimental import pallas as pl
from jax.experimental.pallas import tpu as pltpu
from jax.sharding import PartitionSpec as P

MESH = pl.DeviceIdType.MESH
GATE_LANES = 128


def _route(x, idx, gate, n_pos, n_exp, cap):
    rows = x.shape[0]
    pos = idx // n_exp
    hit = jnp.any(pos[:, None, :] == jnp.arange(n_pos)[None, :, None], axis=-1)
    r = jnp.arange(rows)
    before = (r[None, :] < r[:, None]).astype(jnp.bfloat16)
    rank = jnp.dot(before, hit.astype(jnp.bfloat16), preferred_element_type=jnp.float32).astype(jnp.int32)
    slot = jnp.where(hit, rank, cap)
    sel = slot.T[:, None, :] == jnp.arange(cap)[None, :, None]
    pick = sel.astype(jnp.bfloat16)
    xs = jnp.einsum('qsr,rd->qsd', pick, x, preferred_element_type=jnp.float32).astype(jnp.bfloat16)
    experts = jnp.arange(n_pos * n_exp)
    g = jnp.sum(jnp.where(idx[:, :, None] == experts[None, None, :], gate[:, :, None], 0.0), axis=1)
    hi = lax.reduce_precision(g, 8, 7)
    mid = lax.reduce_precision(g - hi, 8, 7)
    lo = g - hi - mid
    parts = jnp.stack([hi, mid, lo], axis=1).astype(jnp.bfloat16).reshape(rows, 3, n_pos, n_exp)
    gs = jnp.einsum('qsr,rpqe->qspe', pick, parts, preferred_element_type=jnp.float32)
    gs = gs.reshape(n_pos, cap, 3 * n_exp).astype(jnp.bfloat16)
    gs = jnp.pad(gs, ((0, 0), (0, 0), (0, GATE_LANES - 3 * n_exp)))
    return jnp.concatenate([xs, gs], axis=-1), sel


def _kernel(n_pos, n_tp, cap, xs, w1, w3, w2, out, xb, xt, acc, rec, rel, b13, b2,
            wsem, sx, rx, sn, rn, sl, rl, sr, rr, su, ru, sg, rg, sm, rm, sf, rf):
    q = lax.axis_index('ep')
    y = lax.axis_index('tp')
    up = lax.rem(y + 1, n_tp)
    down = lax.rem(y + n_tp - 1, n_tp)
    n_exp, ff, d = w1.shape
    ch = n_pos * cap
    half = ch // 2
    nh = n_pos // 2
    pairs = n_exp // 2

    def remote(src, dst, ssem, rsem, dev):
        return pltpu.make_async_remote_copy(src_ref=src, dst_ref=dst, send_sem=ssem, recv_sem=rsem,
                                            device_id=dev, device_id_type=MESH)

    def weights(e):
        i, r = e // 2, (e % 2) * 2 * ff
        return (pltpu.make_async_copy(w1.at[e], b13.at[i, pl.ds(r, ff)], wsem.at[e, 0]),
                pltpu.make_async_copy(w3.at[e], b13.at[i, pl.ds(r + ff, ff)], wsem.at[e, 1]),
                pltpu.make_async_copy(w2.at[e], b2.at[e], wsem.at[e, 2]))

    barrier = pltpu.get_barrier_semaphore()
    for k in range(1, n_pos):
        pl.semaphore_signal(barrier, inc=1, device_id={'ep': lax.rem(q + k, n_pos)}, device_id_type=MESH)
    for t in (up, down):
        pl.semaphore_signal(barrier, inc=1, device_id={'tp': t}, device_id_type=MESH)

    def load(e, carry):
        for c in weights(e):
            c.start()
        return carry

    lax.fori_loop(0, n_exp, load, 0)
    pl.semaphore_wait(barrier, n_pos + 1)

    def off(b):
        return b if b < nh else n_pos + nh - 1 - b

    def rows(n):
        return pl.ds(n * cap, cap)

    order = [b for r in range(nh) for b in (r, nh + r)]

    def x_send(b):
        to = lax.rem(q + n_pos - off(b), n_pos)
        return remote(xs.at[to], xb.at[0, rows(b)], sx.at[b], rx.at[b], {'ep': to})

    def near(b):
        src = xs.at[q] if b == 0 else xb.at[0, rows(b)]
        if b < nh:
            return remote(src, xb.at[1, rows(nh + b)], sn.at[b], rn.at[b], {'tp': up})
        return remote(src, xb.at[1, rows(b - nh)], sn.at[b], rn.at[b], {'tp': down})

    def late(r, way):
        if way == 0:
            return remote(xb.at[0, rows(r)], xb.at[3, rows(r)], sl.at[r], rl.at[r], {'tp': down})
        return remote(xb.at[0, rows(nh + r)], xb.at[3, rows(nh + r)], sl.at[nh + r], rl.at[nh + r], {'tp': up})

    def relay(r, way):
        if way == 0:
            return remote(xb.at[1, rows(nh + r)], xb.at[2, rows(r)], sr.at[r], rr.at[r], {'tp': up})
        return remote(xb.at[1, rows(r)], xb.at[2, rows(nh + r)], sr.at[nh + r], rr.at[nh + r], {'tp': down})

    def near_got(r, way):
        if way == 0:
            return remote(xb.at[1, rows(nh + r)], xb.at[1, rows(nh + r)], sn.at[r], rn.at[r], {'tp': up})
        return remote(xb.at[1, rows(r)], xb.at[1, rows(r)], sn.at[nh + r], rn.at[nh + r], {'tp': down})

    for b in order[1:]:
        x_send(b).start()
    near(0).start()
    xb[0, rows(0)] = xs[q]
    for b in order[1:]:
        x_send(b).wait_recv()
        near(b).start()

    lane = lax.broadcasted_iota(jnp.int32, (ch, GATE_LANES), 1)

    def unit(u, hook=None):
        acc[u] = jnp.zeros((ch, d), jnp.float32)
        wide = d // 4
        for n in range(4):
            cols = pl.ds(n * wide, wide)
            xt[cols, :] = xb[u, :, cols].T

        def gate(gv, e):
            mine = (lane == e) | (lane == e + n_exp) | (lane == e + 2 * n_exp)
            return jnp.sum(jnp.where(mine, gv, 0.0), axis=1, keepdims=True)

        def pair(i, carry):
            if hook is not None:
                hook(i)
            ab = jnp.dot(b13[i], xt[...], preferred_element_type=jnp.float32)
            gv = xb[u, :, d:d + GATE_LANES].astype(jnp.float32)
            h, g = [], []
            for t in range(2):
                a, b = ab[2 * t * ff:(2 * t + 1) * ff], ab[(2 * t + 1) * ff:(2 * t + 2) * ff]
                h.append((a * jax.nn.sigmoid(a) * b).astype(jnp.bfloat16).T)
                g.append(gate(gv, 2 * i + t))
            for n in range(4):
                cols = pl.ds(n * wide, wide)
                o0 = jnp.dot(h[0], b2[2 * i, :, cols], preferred_element_type=jnp.float32)
                o1 = jnp.dot(h[1], b2[2 * i + 1, :, cols], preferred_element_type=jnp.float32)
                acc[u, :, cols] += g[0] * o0 + g[1] * o1
            return carry

        lax.fori_loop(0, pairs, pair, 0)

    def first(i):
        for t in range(2):
            for c in weights(2 * i + t):
                c.wait()

        @pl.when(i < n_pos)
        def _():
            r = i // 2

            @pl.when(lax.rem(i, 2) == 0)
            def _():
                near_got(r, 0).wait_recv()
                relay(r, 0).start()
                late(r, 0).start()

            @pl.when(lax.rem(i, 2) == 1)
            def _():
                near_got(r, 1).wait_recv()
                relay(r, 1).start()
                late(r, 1).start()

    unit(0, first)
    unit(1)

    def plain(b):
        if b < nh:
            return remote(acc.at[1, rows(nh + b)], rec.at[1, rows(b)], su.at[b], ru.at[b], {'tp': down})
        return remote(acc.at[1, rows(b - nh)], rec.at[0, rows(b)], su.at[b], ru.at[b], {'tp': up})

    def far(b):
        return remote(acc.at[2, rows(b)], rel.at[rows(b)], sg.at[b], rg.at[b], {'tp': up if b < nh else down})

    def merged(b):
        w = 0 if b < nh else 1
        return remote(acc.at[3, rows(b)], rec.at[w, rows(b)], sm.at[b], rm.at[b], {'tp': down if w else up})

    def final(b):
        to = lax.rem(q + off(b), n_pos)
        return remote(acc.at[0, rows(b)], out.at[q], sf.at[b], rf.at[b], {'ep': to})

    back = [b for r in range(nh - 1, -1, -1) for b in (r, nh + r)]
    for b in back:
        plain(b).start()
    for r in range(nh):
        for w in range(2):
            relay(r, w).wait_recv()
    unit(2)
    for b in back:
        far(b).start()
    for r in range(nh):
        for w in range(2):
            late(r, w).wait_recv()
    unit(3)
    for b in back:
        far(b).wait_recv()
        acc[3, rows(b)] += rel[rows(b)]
        merged(b).start()
    for b in back:
        plain(b).wait_recv()
        merged(b).wait_recv()
        acc[0, rows(b)] += rec[0, rows(b)] + rec[1, rows(b)]
        if b:
            final(b).start()
        else:
            out[q] = acc[0, rows(b)]

    for b in range(n_pos):
        near(b).wait_send()
        plain(b).wait_send()
        far(b).wait_send()
        merged(b).wait_send()
        if b:
            x_send(b).wait_send()
            final(b).wait_send()
            final(b).wait_recv()
    for r in range(nh):
        for w in range(2):
            late(r, w).wait_send()
            relay(r, w).wait_send()


def _moe(xs, w1, w3, w2, n_pos, n_tp, cap):
    n_exp, ff, d = w1.shape
    ch = n_pos * cap
    wide = xs.shape[-1]
    dma = pltpu.SemaphoreType.DMA
    vmem = pl.BlockSpec(memory_space=pltpu.VMEM)
    hbm = pl.BlockSpec(memory_space=pl.ANY)
    return pl.pallas_call(
        functools.partial(_kernel, n_pos, n_tp, cap),
        out_shape=jax.ShapeDtypeStruct((n_pos, cap, d), jnp.float32),
        in_specs=[vmem, hbm, hbm, hbm],
        out_specs=vmem,
        scratch_shapes=[
            pltpu.VMEM((4, ch, wide), jnp.bfloat16),
            pltpu.VMEM((d, ch), jnp.bfloat16),
            pltpu.VMEM((4, ch, d), jnp.float32),
            pltpu.VMEM((2, ch, d), jnp.float32),
            pltpu.VMEM((ch, d), jnp.float32),
            pltpu.VMEM((n_exp // 2, 4 * ff, d), jnp.bfloat16),
            pltpu.VMEM((n_exp, ff, d), jnp.bfloat16),
            dma((n_exp, 3)),
        ] + [dma((n_pos,)) for _ in range(16)],
        compiler_params=pltpu.CompilerParams(
            collective_id=0, has_side_effects=True, vmem_limit_bytes=67043328),
    )(xs, w1, w3, w2)


def solution(mesh):
    n_pos, n_tp = mesh.shape['ep'], mesh.shape['tp']
    rows_spec = P(('dp', 'ep', 'tp'), None)

    def body(x, idx, gate, w1, w3, w2):
        rows, d = x.shape
        n_exp = w1.shape[0]
        cap = 2 * rows // n_pos
        xs, sel = _route(x, idx, gate, n_pos, n_exp, cap)
        back = _moe(xs, jnp.swapaxes(w1, 1, 2), jnp.swapaxes(w3, 1, 2), w2, n_pos, n_tp, cap)
        y = jnp.einsum('qsr,qsd->rd', sel.astype(jnp.float32), back,
                       precision=lax.Precision.HIGHEST, preferred_element_type=jnp.float32)
        return y.astype(jnp.bfloat16)

    return jax.shard_map(body, mesh=mesh,
                         in_specs=(rows_spec, rows_spec, rows_spec,
                                   P('ep', None, 'tp'), P('ep', None, 'tp'), P('ep', 'tp', None)),
                         out_specs=rows_spec, check_vma=False)
```

time: 693 us -> 156 us (0.23)
  other arithmetic: 312 us -> 2.2 us
  waiting for transfers between devices: 161 us -> 0 us
  Pallas kernels: 0 us -> 147 us
  local copies, waits for them, and re-layouts: 90.3 us -> 1.8 us
  blocking collectives: 65.8 us -> 0 us
  matrix products: 43.9 us -> 5.07 us
  between operations: 13.8 us -> 0.07 us
    scatter-add x2 -> x0, other arithmetic: 298 us -> none  [the longest x1 227 us: _groups(): counts = jnp.zeros((n_exp + 1,), jnp.int32).at[key].add(1)[:n_exp]]
    reduce_scatter x1 -> x0, waiting for transfers between devices: 160 us -> none  [body(): y = lax.psum_scatter(part, ('ep', 'tp'), scatter_dimension=0, tiled=True)]
    pallas_call x0 -> x1, Pallas kernels: none -> 147 us  [_moe(): pl.pallas_call(functools.partial(_kernel, n_pos, n_tp, cap), out_shape=ja...]
    gather x5 -> x0, local copies, waits for them, and re-layouts: 85.5 us -> none  [the longest x1 41 us: _experts(): xg = x[tok]]
    all_gather x2 -> x0, blocking collectives: 65.8 us -> none  [the longest x1 33 us: body(): ga = lax.all_gather(gate, ('ep', 'tp'), axis=0, tiled=True)]
    dot_general x2 -> x4, matrix products: 43.9 us -> 5.07 us  [the longest x1 3.29 us: body(): jnp.einsum('qsr,qsd->rd', sel.astype(jnp.float32), back, precision=lax.Pr...]
    sort x1 -> x0, other arithmetic: 11.2 us -> none  [_groups(): order = jnp.argsort(key)]
  transfers between devices with their start and end apart: 2 -> 0, of which waited for: 1 -> 0; matrix products, arithmetic and copies ran while one was open for 42% -> 0% of each run, Pallas kernels for 0% -> 0%
where the time goes in v2:
time: 156 us
  Pallas kernels  147 us (94%)
  matrix products  5.07 us (3%)
  other arithmetic  2.2 us (1%)
  local copies, waits for them, and re-layouts  1.8 us (1%)
    pallas_call x1, Pallas kernels, _moe(): pl.pallas_call(functools.partial(_kernel, n_pos, n_tp, cap), out_shape=ja...  147 us
    dot_general x1, matrix products, body(): jnp.einsum('qsr,qsd->rd', sel.astype(jnp.float32), back, precision=lax.Pr...  3.29 us

profile of v2, /device:TPU:97, one launch (start us, length us, event | category | flops | bytes accessed | tf_op | source)
XLA Modules:
  0.0 156.1 jit_solution(1150399783095092442)
XLA Ops:
  0.0 0.7 add_select_fusion
  0.7 0.1 fusion.3
  0.9 0.0 copy-start
  0.9 0.8 copy.16
  1.7 0.8 copy.15
  2.5 0.3 select_reduce_fusion
  2.8 0.1 copy.17
  2.9 0.2 convolution_convert_fusion.1
  3.1 0.1 copy.18
  3.2 0.0 copy-done
  3.2 1.5 convolution_convert_fusion
  4.7 1.1 fusion.2.xs
  5.8 146.9 %shard_map.64 = f32[8,32,2048]{2,1,0:T(8,128)} custom-call(bf16[8,32,2176]{2,1,0:T(8,128)(2,1)} %fusion.2.xs, bf16[16,192,2048]{2,1,0:T(8,128)(2,1)} %bitcast.20, bf16[16,192,2048]{2,1,0:T(8,128)(2,1)} %bitcast.21, bf16[16,192,2048]{2,1,0:T(8,128)(2,1)} %w2.1), custom_call_target="tpu_custom_call" | custom-call | tf_op jit(solution)/shard_map/pallas_call | solution.py:234
  152.8 3.3 %fusion = bf16[128,2048]{1,0:T(8,128)(2,1)} fusion(f32[8,32,2048]{2,1,0:T(8,128)} %shard_map.64, s32[8,128]{1,0:T(8,128)} %copy-done), kind=kOutput, calls=%fused_computation.2 | convolution fusion | flops 805601280 | bytes 2625536 | tf_op jit(solution)/shard_map/qsr,qsd->rd/dot_general | solution.py:264
  (2 shorter events, 0.0 us)
Async XLA Ops:
  0.9 2.4 %copy-start = (s32[8,128]{1,0:T(8,128)}, s32[8,128]{1,0:T(8,128)S(1)}, u32[]{:S(2)}) copy-start(s32[8,128]{1,0:T(8,128)S(1)} %fusion.3) | copy-start | bytes 12292

commit v3 on v2

--- a/solution.py
+++ b/solution.py
@@ -22,19 +22,20 @@
     sel = slot.T[:, None, :] == jnp.arange(cap)[None, :, None]
     pick = sel.astype(jnp.bfloat16)
     xs = jnp.einsum('qsr,rd->qsd', pick, x, preferred_element_type=jnp.float32).astype(jnp.bfloat16)
-    experts = jnp.arange(n_pos * n_exp)
-    g = jnp.sum(jnp.where(idx[:, :, None] == experts[None, None, :], gate[:, :, None], 0.0), axis=1)
+    experts = jnp.arange(n_pos * n_exp)[:, None]
+    ids, gates = idx.T, gate.T
+    g = sum(jnp.where(ids[k][None, :] == experts, gates[k][None, :], 0.0) for k in range(idx.shape[1]))
     hi = lax.reduce_precision(g, 8, 7)
     mid = lax.reduce_precision(g - hi, 8, 7)
     lo = g - hi - mid
-    parts = jnp.stack([hi, mid, lo], axis=1).astype(jnp.bfloat16).reshape(rows, 3, n_pos, n_exp)
-    gs = jnp.einsum('qsr,rpqe->qspe', pick, parts, preferred_element_type=jnp.float32)
+    parts = jnp.stack([hi, mid, lo]).astype(jnp.bfloat16).reshape(3, n_pos, n_exp, rows)
+    gs = jnp.einsum('qsr,pqer->qspe', pick, parts, preferred_element_type=jnp.float32)
     gs = gs.reshape(n_pos, cap, 3 * n_exp).astype(jnp.bfloat16)
     gs = jnp.pad(gs, ((0, 0), (0, 0), (0, GATE_LANES - 3 * n_exp)))
     return jnp.concatenate([xs, gs], axis=-1), sel
 
 
-def _kernel(n_pos, n_tp, cap, xs, w1, w3, w2, out, xb, xt, acc, rec, rel, b13, b2,
+def _kernel(n_pos, n_tp, cap, xs, w1, w3, w2, out, xb, xt, hs, acc, rec, rel, b13, b2,
             wsem, sx, rx, sn, rn, sl, rl, sr, rr, su, ru, sg, rg, sm, rm, sf, rf):
     q = lax.axis_index('ep')
     y = lax.axis_index('tp')
@@ -124,24 +125,35 @@
             mine = (lane == e) | (lane == e + n_exp) | (lane == e + 2 * n_exp)
             return jnp.sum(jnp.where(mine, gv, 0.0), axis=1, keepdims=True)
 
-        def pair(i, carry):
+        def up_proj(i):
             if hook is not None:
                 hook(i)
-            ab = jnp.dot(b13[i], xt[...], preferred_element_type=jnp.float32)
-            gv = xb[u, :, d:d + GATE_LANES].astype(jnp.float32)
-            h, g = [], []
+            return jnp.dot(b13[i], xt[...], preferred_element_type=jnp.float32)
+
+        def hidden(i, ab):
             for t in range(2):
                 a, b = ab[2 * t * ff:(2 * t + 1) * ff], ab[(2 * t + 1) * ff:(2 * t + 2) * ff]
-                h.append((a * jax.nn.sigmoid(a) * b).astype(jnp.bfloat16).T)
-                g.append(gate(gv, 2 * i + t))
+                hs[lax.rem(i, 2), t] = (a * jax.nn.sigmoid(a) * b).astype(jnp.bfloat16).T
+
+        def down_proj(i):
+            gv = xb[u, :, d:d + GATE_LANES].astype(jnp.float32)
+            g0, g1 = gate(gv, 2 * i), gate(gv, 2 * i + 1)
+            p = lax.rem(i, 2)
             for n in range(4):
                 cols = pl.ds(n * wide, wide)
-                o0 = jnp.dot(h[0], b2[2 * i, :, cols], preferred_element_type=jnp.float32)
-                o1 = jnp.dot(h[1], b2[2 * i + 1, :, cols], preferred_element_type=jnp.float32)
-                acc[u, :, cols] += g[0] * o0 + g[1] * o1
+                o0 = jnp.dot(hs[p, 0], b2[2 * i, :, cols], preferred_element_type=jnp.float32)
+                o1 = jnp.dot(hs[p, 1], b2[2 * i + 1, :, cols], preferred_element_type=jnp.float32)
+                acc[u, :, cols] += g0 * o0 + g1 * o1
+
+        def pair(i, carry):
+            ab = up_proj(i + 1)
+            down_proj(i)
+            hidden(i + 1, ab)
             return carry
 
-        lax.fori_loop(0, pairs, pair, 0)
+        hidden(0, up_proj(0))
+        lax.fori_loop(0, pairs - 1, pair, 0)
+        down_proj(pairs - 1)
 
     def first(i):
         for t in range(2):
@@ -239,6 +251,7 @@
         scratch_shapes=[
             pltpu.VMEM((4, ch, wide), jnp.bfloat16),
             pltpu.VMEM((d, ch), jnp.bfloat16),
+            pltpu.VMEM((2, 2, ch, ff), jnp.bfloat16),
             pltpu.VMEM((4, ch, d), jnp.float32),
             pltpu.VMEM((2, ch, d), jnp.float32),
             pltpu.VMEM((ch, d), jnp.float32),

time: 156 us -> 139 us (0.89)
  Pallas kernels: 147 us -> 130 us
    pallas_call x1, Pallas kernels: 147 us -> 130 us  [_moe(): pl.pallas_call(functools.partial(_kernel, n_pos, n_tp, cap), out_shape=ja...]
    slice x0 -> x2, local copies, waits for them, and re-layouts: none -> 1.98 us  [the longest x1 1 us: _route(): gates[k][None, :]]
    unnamed x4 -> x2, local copies, waits for them, and re-layouts: 1.6 us -> 0.01 us
where the time goes in v3:
time: 139 us
  Pallas kernels  130 us (94%)
  matrix products  5.08 us (4%)
  local copies, waits for them, and re-layouts  2.1 us (2%)
  other arithmetic  1.96 us (1%)
    pallas_call x1, Pallas kernels, _moe(): pl.pallas_call(functools.partial(_kernel, n_pos, n_tp, cap), out_shape=ja...  130 us
    dot_general x1, matrix products, body(): jnp.einsum('qsr,qsd->rd', sel.astype(jnp.float32), back, precision=lax.Pr...  3.29 us

profile of v3, /device:TPU:97, one launch (start us, length us, event | category | flops | bytes accessed | tf_op | source)
XLA Modules:
  0.0 138.8 jit_solution(12002033448106773005)
XLA Ops:
  0.0 0.7 add_select_fusion
  0.7 0.1 fusion.3
  0.9 0.0 copy-start
  0.9 1.0 slice_bitcast_fusion.14
  1.9 1.0 slice_bitcast_fusion.15
  2.9 0.1 reduce-precision_convert_fusion.1
  3.0 0.2 convolution_convert_fusion.1
  3.2 0.1 copy.11
  3.3 0.0 copy-done
  3.3 1.5 %convolution_convert_fusion = bf16[8,32,2048]{2,1,0:T(8,128)(2,1)S(1)} fusion(bf16[128,2048]{1,0:T(8,128)(2,1)} %param.6, s32[8,128]{1,0:T(8,128)S(1)} %fusion.3), kind=kOutput, calls=%fused_computation | convolution fusion | flops 134774784 | bytes 1576960 | tf_op jit(solution)/shard_map/qsr,rd->qsd/dot_general | solution.py:24
  4.8 1.1 fusion.2.xs
  5.9 129.6 %shard_map.64 = f32[8,32,2048]{2,1,0:T(8,128)} custom-call(bf16[8,32,2176]{2,1,0:T(8,128)(2,1)} %fusion.2.xs, bf16[16,192,2048]{2,1,0:T(8,128)(2,1)} %bitcast.53, bf16[16,192,2048]{2,1,0:T(8,128)(2,1)} %bitcast.54, bf16[16,192,2048]{2,1,0:T(8,128)(2,1)} %w2.1), custom_call_target="tpu_custom_call" | custom-call | tf_op jit(solution)/shard_map/pallas_call | solution.py:246
  135.5 3.3 %fusion = bf16[128,2048]{1,0:T(8,128)(2,1)} fusion(f32[8,32,2048]{2,1,0:T(8,128)} %shard_map.64, s32[8,128]{1,0:T(8,128)} %copy-done), kind=kOutput, calls=%fused_computation.2 | convolution fusion | flops 805601280 | bytes 2625536 | tf_op jit(solution)/shard_map/qsr,qsd->rd/dot_general | solution.py:277
  (2 shorter events, 0.0 us)
Async XLA Ops:
  0.9 2.4 %copy-start = (s32[8,128]{1,0:T(8,128)}, s32[8,128]{1,0:T(8,128)S(1)}, u32[]{:S(2)}) copy-start(s32[8,128]{1,0:T(8,128)S(1)} %fusion.3) | copy-start | bytes 12292

commit v4 on v3

--- a/solution.py
+++ b/solution.py
@@ -9,10 +9,12 @@
 
 MESH = pl.DeviceIdType.MESH
 GATE_LANES = 128
-
-
-def _route(x, idx, gate, n_pos, n_exp, cap):
-    rows = x.shape[0]
+CODE_MAX = 32700.0
+TINY = 1e-37
+
+
+def _route(idx, gate, n_pos, n_exp, cap):
+    rows = idx.shape[0]
     pos = idx // n_exp
     hit = jnp.any(pos[:, None, :] == jnp.arange(n_pos)[None, :, None], axis=-1)
     r = jnp.arange(rows)
@@ -21,7 +23,6 @@
     slot = jnp.where(hit, rank, cap)
     sel = slot.T[:, None, :] == jnp.arange(cap)[None, :, None]
     pick = sel.astype(jnp.bfloat16)
-    xs = jnp.einsum('qsr,rd->qsd', pick, x, preferred_element_type=jnp.float32).astype(jnp.bfloat16)
     experts = jnp.arange(n_pos * n_exp)[:, None]
     ids, gates = idx.T, gate.T
     g = sum(jnp.where(ids[k][None, :] == experts, gates[k][None, :], 0.0) for k in range(idx.shape[1]))
@@ -32,10 +33,25 @@
     gs = jnp.einsum('qsr,pqer->qspe', pick, parts, preferred_element_type=jnp.float32)
     gs = gs.reshape(n_pos, cap, 3 * n_exp).astype(jnp.bfloat16)
     gs = jnp.pad(gs, ((0, 0), (0, 0), (0, GATE_LANES - 3 * n_exp)))
-    return jnp.concatenate([xs, gs], axis=-1), sel
-
-
-def _kernel(n_pos, n_tp, cap, xs, w1, w3, w2, out, xb, xt, hs, acc, rec, rel, b13, b2,
+    return pick.reshape(n_pos * cap, rows), gs.reshape(n_pos * cap, GATE_LANES)
+
+
+def _encode(v):
+    r, d = v.shape
+    top = jnp.max(jnp.abs(v), axis=1, keepdims=True)
+    e = jnp.ceil(jnp.log2(jnp.maximum(top, TINY)))
+    root = v * lax.rsqrt(jnp.maximum(jnp.abs(v), TINY))
+    code = jnp.round(root * (CODE_MAX * jnp.exp2(-0.5 * e))).astype(jnp.int32).astype(jnp.int16)
+    return code, jnp.broadcast_to(e, (r, 128)).astype(jnp.int32).astype(jnp.int16)
+
+
+def _decode(code, e):
+    e = e.astype(jnp.int32).astype(jnp.float32)[:, 0:1]
+    root = code.astype(jnp.int32).astype(jnp.float32) * (jnp.exp2(0.5 * e) * (1.0 / CODE_MAX))
+    return root * jnp.abs(root)
+
+
+def _kernel(n_pos, n_tp, cap, x, pick, gs, w1, w3, w2, out, xs, xb, xt, hs, acc, cd, rec, rel, fin, b13, b2,
             wsem, sx, rx, sn, rn, sl, rl, sr, rr, su, ru, sg, rg, sm, rm, sf, rf):
     q = lax.axis_index('ep')
     y = lax.axis_index('tp')
@@ -69,6 +85,12 @@
         return carry
 
     lax.fori_loop(0, n_exp, load, 0)
+    wide = d // 4
+    for n in range(4):
+        cols = pl.ds(n * wide, wide)
+        picked = jnp.dot(pick[...], x[:, cols], preferred_element_type=jnp.float32)
+        xs[:, :, cols] = picked.astype(jnp.bfloat16).reshape(n_pos, cap, wide)
+    xs[:, :, d:d + GATE_LANES] = gs[...].reshape(n_pos, cap, GATE_LANES)
     pl.semaphore_wait(barrier, n_pos + 1)
 
     def off(b):
@@ -115,8 +137,8 @@
     lane = lax.broadcasted_iota(jnp.int32, (ch, GATE_LANES), 1)
 
     def unit(u, hook=None):
-        acc[u] = jnp.zeros((ch, d), jnp.float32)
-        wide = d // 4
+        s = min(u, 1)
+        acc[s] = jnp.zeros((ch, d), jnp.float32)
         for n in range(4):
             cols = pl.ds(n * wide, wide)
             xt[cols, :] = xb[u, :, cols].T
@@ -143,7 +165,7 @@
                 cols = pl.ds(n * wide, wide)
                 o0 = jnp.dot(hs[p, 0], b2[2 * i, :, cols], preferred_element_type=jnp.float32)
                 o1 = jnp.dot(hs[p, 1], b2[2 * i + 1, :, cols], preferred_element_type=jnp.float32)
-                acc[u, :, cols] += g0 * o0 + g1 * o1
+                acc[s, :, cols] += g0 * o0 + g1 * o1
 
         def pair(i, carry):
             ab = up_proj(i + 1)
@@ -179,30 +201,39 @@
     unit(0, first)
     unit(1)
 
+    def encode(u, n, v):
+        cd[u, rows(n), 0:d], cd[u, rows(n), d:d + 128] = _encode(v)
+
+    def decode(ref):
+        return _decode(ref[:, 0:d], ref[:, d:d + 128])
+
     def plain(b):
         if b < nh:
-            return remote(acc.at[1, rows(nh + b)], rec.at[1, rows(b)], su.at[b], ru.at[b], {'tp': down})
-        return remote(acc.at[1, rows(b - nh)], rec.at[0, rows(b)], su.at[b], ru.at[b], {'tp': up})
+            return remote(cd.at[1, rows(nh + b)], rec.at[1, rows(b)], su.at[b], ru.at[b], {'tp': down})
+        return remote(cd.at[1, rows(b - nh)], rec.at[0, rows(b)], su.at[b], ru.at[b], {'tp': up})
 
     def far(b):
-        return remote(acc.at[2, rows(b)], rel.at[rows(b)], sg.at[b], rg.at[b], {'tp': up if b < nh else down})
+        return remote(cd.at[2, rows(b)], rel.at[rows(b)], sg.at[b], rg.at[b], {'tp': up if b < nh else down})
 
     def merged(b):
         w = 0 if b < nh else 1
-        return remote(acc.at[3, rows(b)], rec.at[w, rows(b)], sm.at[b], rm.at[b], {'tp': down if w else up})
+        return remote(cd.at[3, rows(b)], rec.at[w, rows(b)], sm.at[b], rm.at[b], {'tp': down if w else up})
 
     def final(b):
         to = lax.rem(q + off(b), n_pos)
-        return remote(acc.at[0, rows(b)], out.at[q], sf.at[b], rf.at[b], {'ep': to})
+        return remote(cd.at[0, rows(b)], fin.at[rows(q)], sf.at[b], rf.at[b], {'ep': to})
 
     back = [b for r in range(nh - 1, -1, -1) for b in (r, nh + r)]
     for b in back:
+        n = nh + b if b < nh else b - nh
+        encode(1, n, acc[1, rows(n)])
         plain(b).start()
     for r in range(nh):
         for w in range(2):
             relay(r, w).wait_recv()
     unit(2)
     for b in back:
+        encode(2, b, acc[1, rows(b)])
         far(b).start()
     for r in range(nh):
         for w in range(2):
@@ -210,16 +241,29 @@
     unit(3)
     for b in back:
         far(b).wait_recv()
-        acc[3, rows(b)] += rel[rows(b)]
+        encode(3, b, acc[1, rows(b)] + decode(rel.at[rows(b)]))
         merged(b).start()
     for b in back:
         plain(b).wait_recv()
         merged(b).wait_recv()
-        acc[0, rows(b)] += rec[0, rows(b)] + rec[1, rows(b)]
+        encode(0, b, acc[0, rows(b)] + decode(rec.at[0, rows(b)]) + decode(rec.at[1, rows(b)]))
         if b:
             final(b).start()
         else:
-            out[q] = acc[0, rows(b)]
+            fin[rows(q)] = cd[0, rows(0)]
+    for b in range(1, n_pos):
+        final(b).wait_recv()
+    place = pick[...].T
+    scale = fin[:, d:d + 128]
+    for n in range(4):
+        cols = pl.ds(n * wide, wide)
+        v = _decode(fin[:, cols], scale)
+        total = jnp.zeros((place.shape[0], wide), jnp.float32)
+        for _ in range(3):
+            t = v.astype(jnp.bfloat16)
+            total += jnp.dot(place, t, preferred_element_type=jnp.float32)
+            v = v - t.astype(jnp.float32)
+        out[:, cols] = total.astype(jnp.bfloat16)
 
     for b in range(n_pos):
         near(b).wait_send()
@@ -229,39 +273,42 @@
         if b:
             x_send(b).wait_send()
             final(b).wait_send()
-            final(b).wait_recv()
     for r in range(nh):
         for w in range(2):
             late(r, w).wait_send()
             relay(r, w).wait_send()
 
 
-def _moe(xs, w1, w3, w2, n_pos, n_tp, cap):
+def _moe(x, pick, gs, w1, w3, w2, n_pos, n_tp, cap):
     n_exp, ff, d = w1.shape
     ch = n_pos * cap
-    wide = xs.shape[-1]
+    wide = d + GATE_LANES
+    coded = d + 128
     dma = pltpu.SemaphoreType.DMA
     vmem = pl.BlockSpec(memory_space=pltpu.VMEM)
     hbm = pl.BlockSpec(memory_space=pl.ANY)
     return pl.pallas_call(
         functools.partial(_kernel, n_pos, n_tp, cap),
-        out_shape=jax.ShapeDtypeStruct((n_pos, cap, d), jnp.float32),
-        in_specs=[vmem, hbm, hbm, hbm],
+        out_shape=jax.ShapeDtypeStruct(x.shape, jnp.bfloat16),
+        in_specs=[vmem, vmem, vmem, hbm, hbm, hbm],
         out_specs=vmem,
         scratch_shapes=[
+            pltpu.VMEM((n_pos, cap, wide), jnp.bfloat16),
             pltpu.VMEM((4, ch, wide), jnp.bfloat16),
             pltpu.VMEM((d, ch), jnp.bfloat16),
             pltpu.VMEM((2, 2, ch, ff), jnp.bfloat16),
-            pltpu.VMEM((4, ch, d), jnp.float32),
             pltpu.VMEM((2, ch, d), jnp.float32),
-            pltpu.VMEM((ch, d), jnp.float32),
+            pltpu.VMEM((4, ch, coded), jnp.int16),
+            pltpu.VMEM((2, ch, coded), jnp.int16),
+            pltpu.VMEM((ch, coded), jnp.int16),
+            pltpu.VMEM((ch, coded), jnp.int16),
             pltpu.VMEM((n_exp // 2, 4 * ff, d), jnp.bfloat16),
             pltpu.VMEM((n_exp, ff, d), jnp.bfloat16),
             dma((n_exp, 3)),
         ] + [dma((n_pos,)) for _ in range(16)],
         compiler_params=pltpu.CompilerParams(
             collective_id=0, has_side_effects=True, vmem_limit_bytes=67043328),
-    )(xs, w1, w3, w2)
+    )(x, pick, gs, w1, w3, w2)
 
 
 def solution(mesh):
@@ -269,14 +316,11 @@
     rows_spec = P(('dp', 'ep', 'tp'), None)
 
     def body(x, idx, gate, w1, w3, w2):
-        rows, d = x.shape
+        rows = x.shape[0]
         n_exp = w1.shape[0]
         cap = 2 * rows // n_pos
-        xs, sel = _route(x, idx, gate, n_pos, n_exp, cap)
-        back = _moe(xs, jnp.swapaxes(w1, 1, 2), jnp.swapaxes(w3, 1, 2), w2, n_pos, n_tp, cap)
-        y = jnp.einsum('qsr,qsd->rd', sel.astype(jnp.float32), back,
-                       precision=lax.Precision.HIGHEST, preferred_element_type=jnp.float32)
-        return y.astype(jnp.bfloat16)
+        pick, gs = _route(idx, gate, n_pos, n_exp, cap)
+        return _moe(x, pick, gs, jnp.swapaxes(w1, 1, 2), jnp.swapaxes(w3, 1, 2), w2, n_pos, n_tp, cap)
 
     return jax.shard_map(body, mesh=mesh,
                          in_specs=(rows_spec, rows_spec, rows_spec,

time: 139 us -> 111 us (0.80)
  Pallas kernels: 130 us -> 104 us
  matrix products: 5.08 us -> 0.32 us
  local copies, waits for them, and re-layouts: 2.1 us -> 4.72 us
    pallas_call x1, Pallas kernels: 130 us -> 104 us  [_moe(): pl.pallas_call(functools.partial(_kernel, n_pos, n_tp, cap), out_shape=ja...]
    dot_general x2 -> x0, matrix products: 4.76 us -> none  [the longest x1 3.29 us: body(): jnp.einsum('qsr,qsd->rd', sel.astype(jnp.float32), back, precision=lax.Pr...]
    unnamed x2 -> x1, local copies, waits for them, and re-layouts: 0.01 us -> 1.88 us
where the time goes in v4:
time: 111 us
  Pallas kernels  104 us (94%)
  local copies, waits for them, and re-layouts  4.72 us (4%)
  other arithmetic  1.59 us (1%)
    pallas_call x1, Pallas kernels, _moe(): pl.pallas_call(functools.partial(_kernel, n_pos, n_tp, cap), out_shape=ja...  104 us

profile of v4, /device:TPU:97, one launch (start us, length us, event | category | flops | bytes accessed | tf_op | source)
XLA Modules:
  0.0 111.1 jit_solution(15719838957294392715)
XLA Ops:
  0.0 0.7 add_select_fusion
  0.7 0.1 fusion
  0.9 0.1 eq.275
  1.0 1.0 slice_bitcast_fusion.14
  2.0 1.0 slice_bitcast_fusion.15
  2.9 0.7 fusion.3.pick
  3.7 0.1 reduce-precision_convert_fusion.1
  3.8 0.2 convolution_convert_fusion
  4.0 0.1 copy.9
  4.1 0.7 pad.4
  4.8 104.5 %shard_map.64 = bf16[128,2048]{1,0:T(8,128)(2,1)} custom-call(bf16[128,2048]{1,0:T(8,128)(2,1)} %x.3, bf16[256,128]{1,0:T(8,128)(2,1)} %fusion.3.pick, bf16[256,128]{1,0:T(8,128)(2,1)} %bitcast.52, bf16[16,192,2048]{2,1,0:T(8,128)(2,1)} %bitcast.50, bf16[16,192,2048]{2,1,0:T(8,128)(2,1)} %bitcast.51, bf16[16,192,2048]{2,1,0:T(8,128)(2,1)} %w2.1), custom_call_target="tpu_custom_call" | custom-call | tf_op jit(solution)/shard_map/pallas_call | solution.py:290
  109.2 1.9 %copy.12 = bf16[128,2048]{1,0:T(8,128)(2,1)} copy(bf16[128,2048]{1,0:T(8,128)(2,1)} %shard_map.64) | data formatting | bytes 1048576
  (3 shorter events, 0.0 us)

commit v5 on v4

v5 whole, which is shorter than its diff:
```python
import functools

import jax
import jax.numpy as jnp
from jax import lax
from jax.experimental import pallas as pl
from jax.experimental.pallas import tpu as pltpu
from jax.sharding import PartitionSpec as P

MESH = pl.DeviceIdType.MESH
GATE_LANES = 128
CODE_MAX = 32700.0
TINY = 1e-37


def _encode(v):
    r, d = v.shape
    top = jnp.max(jnp.abs(v), axis=1, keepdims=True)
    e = jnp.ceil(jnp.log2(jnp.maximum(top, TINY)))
    root = v * lax.rsqrt(jnp.maximum(jnp.abs(v), TINY))
    code = jnp.round(root * (CODE_MAX * jnp.exp2(-0.5 * e))).astype(jnp.int32).astype(jnp.int16)
    return code, jnp.broadcast_to(e, (r, 128)).astype(jnp.int32).astype(jnp.int16)


def _decode(code, e):
    e = e.astype(jnp.int32).astype(jnp.float32)[:, 0:1]
    root = code.astype(jnp.int32).astype(jnp.float32) * (jnp.exp2(0.5 * e) * (1.0 / CODE_MAX))
    return root * jnp.abs(root)


def _route(ids, gates, pick, xs, n_pos, n_exp, cap, d):
    top, rows = ids.shape
    hit = jnp.concatenate(
        [jnp.max(jnp.where((ids[...] >= p * n_exp) & (ids[...] < (p + 1) * n_exp), 1.0, 0.0), axis=0, keepdims=True)
         for p in range(n_pos)], axis=0)
    below = lax.broadcasted_iota(jnp.int32, (rows, rows), 0)
    right = lax.broadcasted_iota(jnp.int32, (rows, rows), 1)
    before = jnp.where(below < right, 1.0, 0.0).astype(jnp.bfloat16)
    rank = jnp.dot(hit.astype(jnp.bfloat16), before, preferred_element_type=jnp.float32)
    slot = jnp.where(hit > 0.0, rank, -1.0).astype(jnp.int32)
    at = lax.broadcasted_iota(jnp.int32, (cap, rows), 0)
    expert = lax.broadcasted_iota(jnp.int32, (n_pos * n_exp, rows), 0)
    g = jnp.zeros((n_pos * n_exp, rows), jnp.float32)
    for k in range(top):
        g += jnp.where(ids[k:k + 1, :] == expert, gates[k:k + 1, :], 0.0)
    terms = []
    for _ in range(3):
        t = g.astype(jnp.bfloat16)
        terms.append(t)
        g = g - t.astype(jnp.float32)
    fill = jnp.zeros((GATE_LANES - 3 * n_exp, rows), jnp.bfloat16)
    for p in range(n_pos):
        one = jnp.where(at == slot[p:p + 1, :], 1.0, 0.0).astype(jnp.bfloat16)
        pick[p * cap:(p + 1) * cap, :] = one
        mine = jnp.concatenate([t[p * n_exp:(p + 1) * n_exp, :] for t in terms] + [fill], axis=0)
        gs = lax.dot_general(one, mine, (((1,), (1,)), ((), ())), preferred_element_type=jnp.float32)
        xs[p, :, d:d + GATE_LANES] = gs.astype(jnp.bfloat16)


def _kernel(n_pos, n_tp, cap, x, ids, gates, w1, w3, w2, out, pick, xs, xb, xt, hs, acc0, acc1, cd0, cd1, cd2, cd3,
            rec, rel, fin, b13, b2,
            wsem, sx, rx, sn, rn, sl, rl, sr, rr, su, ru, sg, rg, sm, rm, sf, rf):
    q = lax.axis_index('ep')
    y = lax.axis_index('tp')
    up = lax.rem(y + 1, n_tp)
    down = lax.rem(y + n_tp - 1, n_tp)
    n_exp, ff, d = w1.shape
    ch = n_pos * cap
    nh = n_pos // 2
    pairs = n_exp // 2

    def remote(src, dst, ssem, rsem, dev):
        return pltpu.make_async_remote_copy(src_ref=src, dst_ref=dst, send_sem=ssem, recv_sem=rsem,
                                            device_id=dev, device_id_type=MESH)

    def weights(e):
        i, r = e // 2, (e % 2) * 2 * ff
        return (pltpu.make_async_copy(w1.at[e], b13.at[i, pl.ds(r, ff)], wsem.at[e, 0]),
                pltpu.make_async_copy(w3.at[e], b13.at[i, pl.ds(r + ff, ff)], wsem.at[e, 1]),
                pltpu.make_async_copy(w2.at[e], b2.at[e], wsem.at[e, 2]))

    barrier = pltpu.get_barrier_semaphore()
    for k in range(1, n_pos):
        pl.semaphore_signal(barrier, inc=1, device_id={'ep': lax.rem(q + k, n_pos)}, device_id_type=MESH)
    for t in (up, down):
        pl.semaphore_signal(barrier, inc=1, device_id={'tp': t}, device_id_type=MESH)

    def load(e, carry):
        for c in weights(e):
            c.start()
        return carry

    lax.fori_loop(0, n_exp, load, 0)
    wide = d // 4
    _route(ids, gates, pick, xs, n_pos, n_exp, cap, d)
    for n in range(4):
        cols = pl.ds(n * wide, wide)
        picked = jnp.dot(pick[...], x[:, cols], preferred_element_type=jnp.float32)
        xs[:, :, cols] = picked.astype(jnp.bfloat16).reshape(n_pos, cap, wide)
    pl.semaphore_wait(barrier, n_pos + 1)

    def off(b):
        return b if b < nh else n_pos + nh - 1 - b

    def rows(n):
        return pl.ds(n * cap, cap)

    early, rest = range(nh // 2), range(nh // 2, nh)
    first4 = [b for r in early for b in (r, nh + r)]
    last4 = [b for r in rest for b in (r, nh + r)]
    units = (
        [('O', b) for b in first4] + [(c, r) for r in early for c in 'AB'],
        [(c, r) for r in rest for c in 'AB'] + [('F', b) for b in first4],
        [('F', b) for b in last4] + [(c, r) for r in early for c in 'CD'],
        [('O', b) for b in last4] + [(c, r) for r in rest for c in 'CD'],
    )
    place = {name: (u, n) for u, names in enumerate(units) for n, name in enumerate(names)}

    def spot(c, r):
        u, n = place[c, r]
        return xb.at[u, rows(n)]

    def x_send(b):
        to = lax.rem(q + n_pos - off(b), n_pos)
        return remote(xs.at[to], spot('O', b), sx.at[b], rx.at[b], {'ep': to})

    def near(b):
        src = xs.at[q] if b == 0 else spot('O', b)
        if b < nh:
            return remote(src, spot('A', b), sn.at[b], rn.at[b], {'tp': up})
        return remote(src, spot('B', b - nh), sn.at[b], rn.at[b], {'tp': down})

    def late(b):
        if b < nh:
            return remote(spot('O', b), spot('C', b), sl.at[b], rl.at[b], {'tp': down})
        return remote(spot('O', b), spot('D', b - nh), sl.at[b], rl.at[b], {'tp': up})

    def relay(b):
        if b < nh:
            return remote(spot('A', b), spot('F', b), sr.at[b], rr.at[b], {'tp': up})
        return remote(spot('B', b - nh), spot('F', b), sr.at[b], rr.at[b], {'tp': down})

    for b in (first4 + last4)[1:]:
        x_send(b).start()
    near(0).start()
    u, n = place['O', 0]
    xb[u, rows(n)] = xs[q]
    for b in first4[1:]:
        x_send(b).wait_recv()
        near(b).start()
    for b in first4:
        near(b).wait_recv()

    lane = lax.broadcasted_iota(jnp.int32, (ch, GATE_LANES), 1)

    def unit(u, acc, hook=None):
        for n in range(4):
            cols = pl.ds(n * wide, wide)
            xt[cols, :] = xb[u, :, cols].T

        def gate(gv, e):
            mine = (lane == e) | (lane == e + n_exp) | (lane == e + 2 * n_exp)
            return jnp.sum(jnp.where(mine, gv, 0.0), axis=1, keepdims=True)

        def up_proj(i):
            if hook is not None:
                hook(i)
            return jnp.dot(b13[i], xt[...], preferred_element_type=jnp.float32)

        def hidden(i, ab):
            for t in range(2):
                a, b = ab[2 * t * ff:(2 * t + 1) * ff], ab[(2 * t + 1) * ff:(2 * t + 2) * ff]
                hs[lax.rem(i, 2), t] = (a * jax.nn.sigmoid(a) * b).astype(jnp.bfloat16).T

        def down_proj(i):
            gv = xb[u, :, d:d + GATE_LANES].astype(jnp.float32)
            g0, g1 = gate(gv, 2 * i), gate(gv, 2 * i + 1)
            p = lax.rem(i, 2)
            for n in range(4):
                cols = pl.ds(n * wide, wide)
                o0 = jnp.dot(hs[p, 0], b2[2 * i, :, cols], preferred_element_type=jnp.float32)
                o1 = jnp.dot(hs[p, 1], b2[2 * i + 1, :, cols], preferred_element_type=jnp.float32)
                acc[:, cols] = jnp.where(i == 0, 0.0, acc[:, cols]) + (g0 * o0 + g1 * o1)

        def pair(i, carry):
            ab = up_proj(i + 1)
            down_proj(i)
            hidden(i + 1, ab)
            return carry

        hidden(0, up_proj(0))
        lax.fori_loop(0, pairs - 1, pair, 0)
        down_proj(pairs - 1)

    def relays(r):
        relay(r).start()
        relay(nh + r).start()

    def nears(r):
        for b in (r, nh + r):
            x_send(b).wait_recv()
            near(b).start()

    def lates(r):
        late(r).start()
        late(nh + r).start()

    def passed(r):
        near(r).wait_recv()
        near(nh + r).wait_recv()
        relays(r)

    todo = [functools.partial(f, r) for f, r in (
        (relays, 0), (nears, 2), (relays, 1), (nears, 3), (lates, 0), (lates, 1), (passed, 2), (passed, 3))]

    def first(i):
        for t in range(2):
            for c in weights(2 * i + t):
                c.wait()
        for step, act in enumerate(todo):
            pl.when(i == step)(act)

    def encode(ref, n, v):
        ref[rows(n), 0:d], ref[rows(n), d:d + 128] = _encode(v)

    def decode(ref):
        return _decode(ref[:, 0:d], ref[:, d:d + 128])

    def mine(c, r):
        u, n = place[c, r]
        return (acc1 if u else acc0)[rows(n), :]

    def plain(b):
        w = 1 if b < nh else 0
        return remote(cd1.at[rows(b)], rec.at[w, rows(b)], su.at[b], ru.at[b], {'tp': down if w else up})

    def far(b):
        return remote(cd2.at[rows(b)], rel.at[rows(b)], sg.at[b], rg.at[b], {'tp': up if b < nh else down})

    def merged(b):
        w = 0 if b < nh else 1
        return remote(cd3.at[rows(b)], rec.at[w, rows(b)], sm.at[b], rm.at[b], {'tp': down if w else up})

    def final(b):
        to = lax.rem(q + off(b), n_pos)
        return remote(cd0.at[rows(b)], fin.at[rows(q)], sf.at[b], rf.at[b], {'ep': to})

    def send_plain(blocks):
        for b in blocks:
            encode(cd1, b, mine('A', b) if b < nh else mine('B', b - nh))
            plain(b).start()

    def send_far(blocks):
        for b in blocks:
            encode(cd2, b, mine('F', b))
            far(b).start()

    def send_merged(blocks):
        for b in blocks:
            far(b).wait_recv()
            own = mine('C', b) if b < nh else mine('D', b - nh)
            encode(cd3, b, own + decode(rel.at[rows(b)]))
            merged(b).start()

    def send_final(blocks):
        for b in blocks:
            plain(b).wait_recv()
            merged(b).wait_recv()
            encode(cd0, b, mine('O', b) + decode(rec.at[0, rows(b)]) + decode(rec.at[1, rows(b)]))
            if b:
                final(b).start()
            else:
                fin[rows(q)] = cd0[rows(0)]

    unit(0, acc0, first)
    send_plain(first4)
    lates(2)
    lates(3)
    for b in first4:
        relay(b).wait_recv()
    unit(1, acc1)
    send_far(first4)
    send_plain(last4)
    for b in last4:
        relay(b).wait_recv()
    for b in first4:
        late(b).wait_recv()
    unit(2, acc1)
    send_far(last4)
    send_merged(first4)
    for b in last4:
        late(b).wait_recv()
    unit(3, acc1)
    send_merged(last4)
    send_final(first4)
    send_final(last4)
    for b in range(1, n_pos):
        final(b).wait_recv()
    home = pick[...].T
    scale = fin[:, d:d + 128]
    for n in range(4):
        cols = pl.ds(n * wide, wide)
        v = _decode(fin[:, cols], scale)
        total = jnp.zeros((home.shape[0], wide), jnp.float32)
        for _ in range(3):
            t = v.astype(jnp.bfloat16)
            total += jnp.dot(home, t, preferred_element_type=jnp.float32)
            v = v - t.astype(jnp.float32)
        out[:, cols] = total.astype(jnp.bfloat16)

    for b in range(n_pos):
        near(b).wait_send()
        late(b).wait_send()
        relay(b).wait_send()
        plain(b).wait_send()
        far(b).wait_send()
        merged(b).wait_send()
        if b:
            x_send(b).wait_send()
            final(b).wait_send()


def _moe(x, ids, gates, w1, w3, w2, n_pos, n_tp, cap):
    n_exp, ff, d = w1.shape
    ch = n_pos * cap
    wide = d + GATE_LANES
    coded = d + 128
    dma = pltpu.SemaphoreType.DMA
    vmem = pl.BlockSpec(memory_space=pltpu.VMEM)
    hbm = pl.BlockSpec(memory_space=pl.ANY)
    return pl.pallas_call(
        functools.partial(_kernel, n_pos, n_tp, cap),
        out_shape=jax.ShapeDtypeStruct(x.shape, jnp.bfloat16),
        in_specs=[vmem, vmem, vmem, hbm, hbm, hbm],
        out_specs=vmem,
        scratch_shapes=[
            pltpu.VMEM((ch, x.shape[0]), jnp.bfloat16),
            pltpu.VMEM((n_pos, cap, wide), jnp.bfloat16),
            pltpu.VMEM((4, ch, wide), jnp.bfloat16),
            pltpu.VMEM((d, ch), jnp.bfloat16),
            pltpu.VMEM((2, 2, ch, ff), jnp.bfloat16),
            pltpu.VMEM((ch, d), jnp.float32),
            pltpu.VMEM((ch, d), jnp.float32),
            pltpu.VMEM((ch, coded), jnp.int16),
            pltpu.VMEM((ch, coded), jnp.int16),
            pltpu.VMEM((ch, coded), jnp.int16),
            pltpu.VMEM((ch, coded), jnp.int16),
            pltpu.VMEM((2, ch, coded), jnp.int16),
            pltpu.VMEM((ch, coded), jnp.int16),
            pltpu.VMEM((ch, coded), jnp.int16),
            pltpu.VMEM((n_exp // 2, 4 * ff, d), jnp.bfloat16),
            pltpu.VMEM((n_exp, ff, d), jnp.bfloat16),
            dma((n_exp, 3)),
        ] + [dma((n_pos,)) for _ in range(16)],
        compiler_params=pltpu.CompilerParams(
            collective_id=0, has_side_effects=True, vmem_limit_bytes=67043328),
    )(x, ids, gates, w1, w3, w2)


def solution(mesh):
    n_pos, n_tp = mesh.shape['ep'], mesh.shape['tp']
    rows_spec = P(('dp', 'ep', 'tp'), None)

    def body(x, idx, gate, w1, w3, w2):
        rows = x.shape[0]
        cap = 2 * rows // n_pos
        return _moe(x, idx.T, gate.T, jnp.swapaxes(w1, 1, 2), jnp.swapaxes(w3, 1, 2), w2, n_pos, n_tp, cap)

    return jax.shard_map(body, mesh=mesh,
                         in_specs=(rows_spec, rows_spec, rows_spec,
                                   P('ep', None, 'tp'), P('ep', None, 'tp'), P('ep', 'tp', None)),
                         out_specs=rows_spec, check_vma=False)
```

time: 111 us -> 103 us (0.928); the launches traced: 111 us -> 102 us
  Pallas kernels: 104 us -> 99.8 us
  local copies, waits for them, and re-layouts: 4.72 us -> 1.88 us
  other arithmetic: 1.59 us -> 0 us
    pallas_call x1, Pallas kernels: 104 us -> 99.8 us  [_moe(): pl.pallas_call(functools.partial(_kernel, n_pos, n_tp, cap), out_shape=ja...]
    slice x2 -> x0, local copies, waits for them, and re-layouts: 1.98 us -> none  [the longest x1 0.99 us: _route(): gates[k][None, :]]
where the time goes in v5:
time: 103 us; the launch traced here: 102 us
  Pallas kernels  99.8 us (97%)
  local copies, waits for them, and re-layouts  1.88 us (2%)
    pallas_call x1, Pallas kernels, _moe(): pl.pallas_call(functools.partial(_kernel, n_pos, n_tp, cap), out_shape=ja...  99.8 us

profile of v5, /device:TPU:97, one launch (start us, length us, event | category | flops | bytes accessed | tf_op | source)
XLA Modules:
  0.0 101.7 jit_solution(6131225217735316647)
XLA Ops:
  0.0 99.8 %shard_map.64 = bf16[128,2048]{1,0:T(8,128)(2,1)} custom-call(bf16[128,2048]{1,0:T(8,128)(2,1)} %x.1, s32[8,128]{1,0:T(8,128)} %bitcast.6, f32[8,128]{1,0:T(8,128)} %bitcast.7, bf16[16,192,2048]{2,1,0:T(8,128)(2,1)} %bitcast.4, bf16[16,192,2048]{2,1,0:T(8,128)(2,1)} %bitcast.5, bf16[16,192,2048]{2,1,0:T(8,128)(2,1)} %w2.1), custom_call_target="tpu_custom_call" | custom-call | tf_op jit(solution)/shard_map/pallas_call | solution.py:331
  99.8 1.9 %copy.8 = bf16[128,2048]{1,0:T(8,128)(2,1)} copy(bf16[128,2048]{1,0:T(8,128)(2,1)} %shard_map.64) | data formatting | bytes 1048576
